TPU v7x, 32 devices: a whole 2x2x4 slice. The times are simulated.
32 devices in a mesh: rows: 32 (over z, y, x, core).
Axes of the slice: x: 2, y: 2, z: 4, core: 2. Of those that a mesh axis runs over, the one named last changes fastest.
Arguments:
- points: float32 [8, 131072], P(None, 'rows'), may hold values from -6 to 6
- scales: float32 [8], replicated, may hold values from 1 to 3
- noise_var: float32 [131072], P('rows'), may hold values from 0.05 to 0.5
- pivots: int32 [8, 16], replicated, may hold values from 0 to 131071, as said below
Outputs:
- factor: float32 [128, 131072], P(None, 'rows')
- residual_diag: float32 [131072], P('rows')
- mean_residual: float32 [8], replicated
Inputs may be any that keep to these rules, and one draw needn't show every extreme that they name: `pivots`: all 128 entries are distinct point indices.
All inputs are finite; a program needn't handle non-finite values.
Results may differ from a plain program's by a relative error of at most 0.00014.
Values sent between devices are 32-bit elements; how exact they have to be, the bound alone decides.
A program may use at most 64 MiB of HBM per device.

v0:
```python
import jax
import jax.numpy as jnp
from jax import lax
from jax.sharding import PartitionSpec as P


def kernel(first_coords, second_coords):
    summed = jnp.zeros((first_coords.shape[1], second_coords.shape[1]), jnp.float32)
    for axis_pos in range(first_coords.shape[0]):
        differ = first_coords[axis_pos][:, None] - second_coords[axis_pos][None, :]
        summed = summed + differ * differ
    return jnp.exp(-0.5 * summed)


def pick_owned(values, wanted, offset):
    point_count = values.shape[-1]
    owned_mask = ((wanted >= offset) & (wanted < offset + point_count)).astype(jnp.float32)
    position = jnp.clip(wanted - offset, 0, point_count - 1)
    return jnp.take(values, position, axis=values.ndim - 1) * owned_mask


def body(points, scales, noise_var, pivots):
    point_count = points.shape[1]
    blocks, block_rows = pivots.shape
    rank_rows = blocks * block_rows
    total_points = point_count * lax.axis_size("rows")
    scaled = points / scales[:, None]
    offset = lax.axis_index("rows") * point_count
    local_ids = offset + lax.iota(jnp.int32, point_count)
    wanted_all = pivots.reshape(-1)
    coords_all, noise_all = lax.psum(
        (pick_owned(scaled, wanted_all, offset), pick_owned(noise_var, wanted_all, offset)), "rows"
    )
    chol_all = jnp.linalg.cholesky(kernel(coords_all, coords_all) + jnp.diag(noise_all))

    def one_block(block_idx, state_tuple):
        factor, residual_diag, averages = state_tuple
        filled = block_idx * block_rows
        wanted = lax.dynamic_index_in_dim(pivots, block_idx, 0, keepdims=False)
        pivot_coords = lax.dynamic_slice_in_dim(coords_all, filled, block_rows, 1)
        band_rows = lax.dynamic_slice_in_dim(chol_all, filled, block_rows, 0)
        chol_block = lax.dynamic_slice_in_dim(band_rows, filled, block_rows, 1)
        update = jnp.einsum(
            "pr,rn->pn",
            band_rows,
            factor,
            precision=lax.Precision.HIGHEST,
            preferred_element_type=jnp.float32,
        )
        columns = kernel(pivot_coords, scaled) + jnp.where(
            local_ids[None, :] == wanted[:, None], noise_var[None, :], 0.0
        )
        columns = columns - update
        new_rows = lax.linalg.triangular_solve(chol_block, columns, left_side=True, lower=True)
        factor = lax.dynamic_update_slice_in_dim(factor, new_rows, filled, 0)
        residual_diag = residual_diag - jnp.sum(new_rows * new_rows, axis=0)
        local_sum = jnp.sum(residual_diag)
        averages = averages.at[block_idx].set(lax.psum(local_sum, "rows") / total_points)
        return (factor, residual_diag, averages)

    start_state = (
        jnp.zeros((rank_rows, point_count), jnp.float32),
        1.0 + noise_var,
        jnp.zeros((blocks,), jnp.float32),
    )
    factor, residual_diag, averages = lax.fori_loop(0, blocks, one_block, start_state)
    return (factor, residual_diag, averages)


def solution(mesh):
    in_specs = (P(None, "rows"), P(), P("rows"), P())
    out_specs = (P(None, "rows"), P("rows"), P())
    return jax.shard_map(body, mesh=mesh, in_specs=in_specs, out_specs=out_specs, check_vma=False)
```

profile of v0, /device:TPU:0, one launch (start us, length us, event | category | flops | bytes accessed | tf_op | source)
XLA Modules:
  0.0 432.6 jit_solution(481611586461729299)
XLA Ops:
  0.6 0.7 compare_and_fusion
  1.4 0.7 subtract_clamp_fusion
  2.2 1.6 gather_fusion.1
  4.0 2.8 copy.10
  6.8 1.7 broadcast_divide_fusion
  8.6 0.6 gather_fusion
  9.3 42.7 %all-reduce = (f32[128]{0:T(128)S(1)}, f32[8,128]{0,1:T(8,128)S(1)}) all-reduce(f32[128]{0:T(128)S(1)} %get-tuple-element.373, f32[8,128]{0,1:T(8,128)S(1)} %multiply_bitcast_fusion), channel_id=1, replica_groups=mesh['rows'=32] {'rows'}, use_global_device_ids=true, to_apply=%region_1.2 | all-reduce | flops 1152 | bytes 9216 | tf_op jit(solution)/shard_map/psum | solution.py:31
  52.6 11.7 %cholesky.19 = f32[128,128]{1,0:T(8,128)S(1)} custom-call(f32[128,128]{1,0:T(8,128)S(1)} %add_multiply_fusion), custom_call_target="Cholesky" | custom-call | tf_op jit(solution)/shard_map/jit(cholesky)/cholesky | solution.py:34
  64.3 0.6 compare_reduce_fusion
  65.0 0.7 select_select_fusion
  66.5 364.7 %while.22 = (s32[]{:T(128)}, f32[128,4096]{1,0:T(8,128)S(1)}, f32[4096]{0:T(1024)S(1)}, f32[8]{0:T(128)S(1)}, f32[128,128]{1,0:T(8,128)S(1)}, /*index=5*/f32[8,1...) while((s32[]{:T(128)}, f32[128,4096]{1,0:T(8,128)S(1)}, ...), condition=%wide.region_8.9_spmd.clone, body=%wide.region_4.8_spmd.clone.sunk | while | flops 115221000 | bytes 3417065 | solution.py:66
  66.7 0.7 fusion.22
  67.4 1.2 convolution_subtract_fusion.2
  68.7 1.2 custom-call.20
  70.4 0.6 fusion.23
  71.0 40.3 %psum.33 = f32[]{:T(128)} all-reduce(f32[]{:T(128)} %get-tuple-element.493), channel_id=1, replica_groups=mesh['rows'=32] {'rows'}, use_global_device_ids=true, to_apply=%region_7.7 | all-reduce | flops 1 | bytes 8 | tf_op jit(solution)/shard_map/while/body/eval_jaxpr/psum | solution.py:58
  112.3 0.7 fusion.22
  113.0 1.2 convolution_subtract_fusion.2
  114.2 1.2 custom-call.20
  115.9 0.6 fusion.23
  116.5 40.3 %psum.33 = f32[]{:T(128)} all-reduce(f32[]{:T(128)} %get-tuple-element.493), channel_id=1, replica_groups=mesh['rows'=32] {'rows'}, use_global_device_ids=true, to_apply=%region_7.7 | all-reduce | flops 1 | bytes 8 | tf_op jit(solution)/shard_map/while/body/eval_jaxpr/psum | solution.py:58
  157.8 0.7 fusion.22
  158.5 1.2 convolution_subtract_fusion.2
  159.8 1.2 custom-call.20
  161.5 0.6 fusion.23
  162.1 40.4 %psum.33 = f32[]{:T(128)} all-reduce(f32[]{:T(128)} %get-tuple-element.493), channel_id=1, replica_groups=mesh['rows'=32] {'rows'}, use_global_device_ids=true, to_apply=%region_7.7 | all-reduce | flops 1 | bytes 8 | tf_op jit(solution)/shard_map/while/body/eval_jaxpr/psum | solution.py:58
  203.5 0.7 fusion.22
  204.2 1.2 convolution_subtract_fusion.2
  205.5 1.2 custom-call.20
  207.2 0.6 fusion.23
  207.8 40.2 %psum.33 = f32[]{:T(128)} all-reduce(f32[]{:T(128)} %get-tuple-element.493), channel_id=1, replica_groups=mesh['rows'=32] {'rows'}, use_global_device_ids=true, to_apply=%region_7.7 | all-reduce | flops 1 | bytes 8 | tf_op jit(solution)/shard_map/while/body/eval_jaxpr/psum | solution.py:58
  249.0 0.7 fusion.22
  249.7 1.2 convolution_subtract_fusion.2
  251.0 1.2 custom-call.20
  253.3 40.6 %psum.33 = f32[]{:T(128)} all-reduce(f32[]{:T(128)} %get-tuple-element.493), channel_id=1, replica_groups=mesh['rows'=32] {'rows'}, use_global_device_ids=true, to_apply=%region_7.7 | all-reduce | flops 1 | bytes 8 | tf_op jit(solution)/shard_map/while/body/eval_jaxpr/psum | solution.py:58
  294.9 0.7 fusion.22
  295.6 1.2 convolution_subtract_fusion.2
  296.9 1.2 custom-call.20
  299.2 40.0 %psum.33 = f32[]{:T(128)} all-reduce(f32[]{:T(128)} %get-tuple-element.493), channel_id=1, replica_groups=mesh['rows'=32] {'rows'}, use_global_device_ids=true, to_apply=%region_7.7 | all-reduce | flops 1 | bytes 8 | tf_op jit(solution)/shard_map/while/body/eval_jaxpr/psum | solution.py:58
  340.2 0.7 fusion.22
  340.9 1.2 convolution_subtract_fusion.2
  342.2 1.2 custom-call.20
  344.5 40.6 %psum.33 = f32[]{:T(128)} all-reduce(f32[]{:T(128)} %get-tuple-element.493), channel_id=1, replica_groups=mesh['rows'=32] {'rows'}, use_global_device_ids=true, to_apply=%region_7.7 | all-reduce | flops 1 | bytes 8 | tf_op jit(solution)/shard_map/while/body/eval_jaxpr/psum | solution.py:58
  386.2 0.7 fusion.22
  386.9 1.2 convolution_subtract_fusion.2
  388.1 1.2 custom-call.20
  390.4 40.0 %psum.33 = f32[]{:T(128)} all-reduce(f32[]{:T(128)} %get-tuple-element.493), channel_id=1, replica_groups=mesh['rows'=32] {'rows'}, use_global_device_ids=true, to_apply=%region_7.7 | all-reduce | flops 1 | bytes 8 | tf_op jit(solution)/shard_map/while/body/eval_jaxpr/psum | solution.py:58
  431.3 1.3 copy-done
  (85 shorter events, 11.4 us)
Async XLA Ops:
  0.6 6.2 %copy-start.4 = (f32[8]{0:T(128)S(1)}, f32[8]{0:T(128)}, u32[]{:S(2)}) copy-start(f32[8]{0:T(128)} %param.9) | copy-start | bytes 100
  8.5 57.7 %copy-start.1 = (f32[4096]{0:T(1024)S(1)}, f32[4096]{0:T(1024)}, u32[]{:S(2)}) copy-start(f32[4096]{0:T(1024)} %param.10) | copy-start | bytes 49156
  431.3 1.3 copy-start
  431.3 1.3 copy-start.2
  431.3 1.3 copy-start.3
where the time goes:
time: 435 us; the launch traced here: 433 us
  blocking collectives  365 us (84%)
  other arithmetic  33.3 us (8%)
  local copies, waits for them, and re-layouts  14.9 us (3%)
  matrix products  13.1 us (3%)
  loops' own time  5.49 us (1%)
    psum x8, blocking collectives, one_block(): lax.psum(local_sum, 'rows') / total_points  322 us
    psum x1, blocking collectives, body(): lax.psum((pick_owned(scaled, wanted_all, offset), pick_owned(noise_var, w...  42.7 us
    another operation x3, other arithmetic, body(): jnp.linalg.cholesky(kernel(coords_all, coords_all) + jnp.diag(noise_all))  12.4 us
    another operation x16, other arithmetic, one_block(): lax.linalg.triangular_solve(chol_block, columns, left_side=True, lower=True)  10.5 us
    dot_general x8, matrix products, one_block(): jnp.einsum('pr,rn->pn', band_rows, factor, precision=lax.Precision.HIGHES...  9.48 us

commit v1 on v0

v1 whole, which is shorter than its diff:
```python
import functools

import jax
import jax.numpy as jnp
from jax import lax
from jax.experimental import pallas as pl
from jax.experimental.pallas import tpu as pltpu
from jax.sharding import PartitionSpec as P

LANES = 128
SUB = 8
F32 = jnp.float32
BF16 = jnp.bfloat16


def split3(x):
    high = x.astype(BF16).astype(F32)
    rest = x - high
    mid = rest.astype(BF16).astype(F32)
    low = (rest - mid).astype(BF16).astype(F32)
    return high, mid, low


def load_points(dim, points, scales, noise, packed):
    packed[0:dim, :] = points[...] / scales[...]
    packed[dim : 2 * dim, :] = jnp.broadcast_to(noise[...], (dim, noise.shape[1]))


def gather_own(ranks, offset, chunk, pivot_row, packed):
    rows, width = packed.shape
    wanted = pivot_row[...] - offset
    acc = jnp.zeros((3 * rows, ranks), F32)
    for c in range(width // chunk):
        pieces = jnp.concatenate(split3(packed[:, c * chunk : (c + 1) * chunk]), axis=0)
        ids = lax.broadcasted_iota(jnp.int32, (chunk, ranks), 0) + c * chunk
        hot = jnp.where(ids == wanted, 1.0, 0.0).astype(BF16)
        acc = acc + jnp.dot(pieces.astype(BF16), hot, preferred_element_type=F32)
    return acc[0:rows] + acc[rows : 2 * rows] + acc[2 * rows :]


def exchange_start(n, me, slots, send_sem, recv_sem):
    def send(k, carry):
        pltpu.make_async_remote_copy(
            src_ref=slots.at[0],
            dst_ref=slots.at[k],
            send_sem=send_sem.at[k],
            recv_sem=recv_sem.at[k],
            device_id=(lax.rem(me + k, n),),
            device_id_type=pl.DeviceIdType.MESH,
        ).start()
        return carry

    lax.fori_loop(1, n, send, 0)


def exchange_finish(n, me, slots, send_sem, recv_sem):
    def collect(k, total):
        pltpu.make_async_remote_copy(
            src_ref=slots.at[0],
            dst_ref=slots.at[k],
            send_sem=send_sem.at[k],
            recv_sem=recv_sem.at[k],
            device_id=(lax.rem(me + k, n),),
            device_id_type=pl.DeviceIdType.MESH,
        ).wait()
        return total + slots[k]

    return lax.fori_loop(1, n, collect, slots[0])


def pivot_covariance(dim, coords):
    ranks = coords.shape[1]
    across = coords.T
    total = jnp.zeros((ranks, ranks), F32)
    for d in range(dim):
        differ = across[:, d : d + 1] - coords[d : d + 1, :]
        total = total + differ * differ
    row = lax.broadcasted_iota(jnp.int32, (ranks, ranks), 0)
    col = lax.broadcasted_iota(jnp.int32, (ranks, ranks), 1)
    cov = jnp.exp(-0.5 * total) + jnp.where(row == col, coords[dim : dim + 1, :], 0.0)
    return cov, (row == col).astype(F32)


def factor_rows(ranks, state):
    for b in range(ranks // SUB):
        lo, hi = b * SUB, (b + 1) * SUB
        left = [state[lo + i : lo + i + 1, 0:ranks] for i in range(SUB)]
        right = [state[lo + i : lo + i + 1, ranks : 2 * ranks] for i in range(SUB)]
        a = [
            [jnp.broadcast_to(left[i][:, lo + j : lo + j + 1], (1, ranks)) for j in range(i + 1)]
            for i in range(SUB)
        ]
        for k in range(SUB):
            r = lax.rsqrt(a[k][k])
            left[k] = left[k] * r
            right[k] = right[k] * r
            mult = {i: a[i][k] * r for i in range(k + 1, SUB)}
            for i in range(k + 1, SUB):
                for j in range(k + 1, i + 1):
                    a[i][j] = a[i][j] - mult[i] * mult[j]
                left[i] = left[i] - mult[i] * left[k]
                right[i] = right[i] - mult[i] * right[k]
        new_left = jnp.concatenate(left, axis=0)
        new_right = jnp.concatenate(right, axis=0)
        state[lo:hi, 0:ranks] = new_left
        state[lo:hi, ranks : 2 * ranks] = new_right
        if hi < ranks:
            new = jnp.concatenate([new_left, new_right], axis=1)
            h, m, l = split3(new)
            lh, lm, ll = (x[:, 0:ranks] for x in (h, m, l))
            one = jnp.concatenate([lh, lh, lh, lm, lm, ll], axis=0).T[hi:ranks].astype(BF16)
            two = jnp.concatenate([h, m, l, h, m, h], axis=0).astype(BF16)
            state[hi:ranks, :] = state[hi:ranks, :] - jnp.dot(
                one, two, preferred_element_type=F32
            )


def pivot_side(dim, coords, centre):
    y = coords[0:dim, :] - centre
    yh, ym, yl = split3(y)
    nh, nm, nl = split3(-0.5 * jnp.sum(y * y, axis=0, keepdims=True))
    ones = jnp.ones_like(nh)
    tail = [ones, ones, ones, nh, nm, nl, jnp.zeros((dim - 6, y.shape[1]), F32)]
    return jnp.concatenate([yh, yh, ym, ym, yh, yl] + tail, axis=0).T.astype(BF16)


def point_side(dim, x):
    xh, xm, xl = split3(x)
    nh, nm, nl = split3(-0.5 * jnp.sum(x * x, axis=0, keepdims=True))
    ones = jnp.ones_like(nh)
    tail = [nh, nm, nl, ones, ones, ones, jnp.zeros((dim - 6, x.shape[1]), F32)]
    return jnp.concatenate([xh, xm, xh, xm, xl, xh] + tail, axis=0).astype(BF16)


def body_kernel(
    n, blocks, chunk,
    points, scales, noise, pivot_row, pivot_col,
    factor, residual, averages,
    packed, slots, state, held, after, sum_slots,
    send_sem, recv_sem, sum_send_sem, sum_recv_sem, out_sem,
):
    dim, width = points.shape
    ranks = held.shape[0]
    per_block = ranks // blocks
    me = lax.axis_index("rows")
    offset = me * width

    barrier = pltpu.get_barrier_semaphore()

    def greet(k, carry):
        pl.semaphore_signal(
            barrier, inc=1, device_id=(lax.rem(me + k, n),),
            device_id_type=pl.DeviceIdType.MESH,
        )
        return carry

    lax.fori_loop(1, n, greet, 0)
    load_points(dim, points, scales, noise, packed)
    slots[0] = gather_own(ranks, offset, chunk, pivot_row, packed)
    pl.semaphore_wait(barrier, n - 1)
    exchange_start(n, me, slots, send_sem, recv_sem)
    coords = exchange_finish(n, me, slots, send_sem, recv_sem)

    cov, eye = pivot_covariance(dim, coords)
    state[:, 0:ranks] = cov
    state[:, ranks : 2 * ranks] = eye
    factor_rows(ranks, state)
    row = lax.broadcasted_iota(jnp.int32, (ranks, ranks), 0)
    col = lax.broadcasted_iota(jnp.int32, (ranks, ranks), 1)
    solve = jnp.where(row >= col, state[:, ranks : 2 * ranks], 0.0)

    centre = jnp.sum(coords[0:dim, :], axis=1, keepdims=True) / ranks
    side = pivot_side(dim, coords, centre)
    local_col = pivot_col[...] - offset
    copies = []
    for c in range(width // chunk):
        at = slice(c * chunk, (c + 1) * chunk)
        x = packed[0:dim, at] - centre
        cross = jnp.exp(jnp.dot(side, point_side(dim, x), preferred_element_type=F32))
        noise_row = packed[dim : dim + 1, at]
        ids = lax.broadcasted_iota(jnp.int32, (ranks, chunk), 1) + c * chunk
        cross = cross + jnp.where(ids == local_col, noise_row, 0.0)
        rows = jnp.dot(
            solve, cross, precision=lax.Precision.HIGHEST, preferred_element_type=F32
        )
        held[:, at] = rows
        copies.append(
            pltpu.make_async_copy(held.at[:, at], factor.at[:, at], out_sem.at[c])
        )
        copies[-1].start()
        left = 1.0 + noise_row
        for b in range(blocks):
            part = rows[b * per_block : (b + 1) * per_block]
            left = left - jnp.sum(part * part, axis=0, keepdims=True)
            after[b : b + 1, at] = left
        residual[:, at] = left

    total = jnp.zeros((blocks, LANES), F32)
    for c in range(width // LANES):
        total = total + after[:, c * LANES : (c + 1) * LANES]
    sum_slots[0] = total
    exchange_start(n, me, sum_slots, sum_send_sem, sum_recv_sem)
    total = exchange_finish(n, me, sum_slots, sum_send_sem, sum_recv_sem)
    total = jnp.sum(total, axis=1, keepdims=True) / (width * n)
    row = lax.broadcasted_iota(jnp.int32, (blocks, LANES), 0)
    col = lax.broadcasted_iota(jnp.int32, (blocks, LANES), 1)
    averages[...] = jnp.sum(jnp.where(row == col, total, 0.0), axis=0, keepdims=True)[:, 0:blocks]
    for copy in copies:
        copy.wait()


def body(n, points, scales, noise_var, pivots):
    dim, width = points.shape
    blocks, per_block = pivots.shape
    ranks = blocks * per_block
    chunk = 512
    vmem = pl.BlockSpec(memory_space=pltpu.VMEM)
    flat = pivots.reshape(-1)
    factor, residual, averages = pl.pallas_call(
        functools.partial(body_kernel, n, blocks, chunk),
        name="whole",
        out_shape=(
            jax.ShapeDtypeStruct((ranks, width), F32),
            jax.ShapeDtypeStruct((1, width), F32),
            jax.ShapeDtypeStruct((1, blocks), F32),
        ),
        in_specs=[vmem] * 5,
        out_specs=(pl.BlockSpec(memory_space=pl.ANY), vmem, vmem),
        scratch_shapes=[
            pltpu.VMEM((2 * dim, width), F32),
            pltpu.VMEM((n, 2 * dim, ranks), F32),
            pltpu.VMEM((ranks, 2 * ranks), F32),
            pltpu.VMEM((ranks, width), F32),
            pltpu.VMEM((blocks, width), F32),
            pltpu.VMEM((n, blocks, LANES), F32),
            pltpu.SemaphoreType.DMA((n,)),
            pltpu.SemaphoreType.DMA((n,)),
            pltpu.SemaphoreType.DMA((n,)),
            pltpu.SemaphoreType.DMA((n,)),
            pltpu.SemaphoreType.DMA((width // chunk,)),
        ],
        compiler_params=pltpu.CompilerParams(collective_id=0, has_side_effects=True),
    )(
        points, scales.reshape(-1, 1), noise_var.reshape(1, -1),
        flat.reshape(1, -1), flat.reshape(-1, 1),
    )
    return factor, residual.reshape(-1), averages.reshape(-1)


def solution(mesh):
    in_specs = (P(None, "rows"), P(), P("rows"), P())
    out_specs = (P(None, "rows"), P("rows"), P())
    return jax.shard_map(
        functools.partial(body, mesh.shape["rows"]),
        mesh=mesh, in_specs=in_specs, out_specs=out_specs, check_vma=False,
    )
```

time: 435 us -> 41.2 us (0.09)
  blocking collectives: 365 us -> 0 us
  other arithmetic: 33.3 us -> 0 us
  Pallas kernels: 0 us -> 32 us
  matrix products: 13.1 us -> 0 us
  local copies, waits for them, and re-layouts: 14.9 us -> 8.24 us
  loops' own time: 5.49 us -> 0 us
    psum x9 -> x0, blocking collectives: 365 us -> none  [the longest x8 322 us: one_block(): lax.psum(local_sum, 'rows') / total_points]
    pallas_call x0 -> x1, Pallas kernels: none -> 32 us  [body(): pl.pallas_call(functools.partial(body_kernel, n, blocks, chunk), name='wh...]
    another operation x19 -> x0, other arithmetic: 22.9 us -> none  [the longest x3 12.4 us: body(): jnp.linalg.cholesky(kernel(coords_all, coords_all) + jnp.diag(noise_all))]
    dot_general x8 -> x0, matrix products: 9.48 us -> none  [one_block(): jnp.einsum('pr,rn->pn', band_rows, factor, precision=lax.Precision.HIGHES...]
    eq x8 -> x0, local copies, waits for them, and re-layouts: 5.58 us -> none  [one_block(): local_ids[None, :] == wanted[:, None]]
    another operation x1 -> x0, loops' own time: 5.49 us -> none  [body(): lax.fori_loop(0, blocks, one_block, start_state)]
    reduce_sum x8 -> x0, other arithmetic: 4.9 us -> none  [one_block(): local_sum = jnp.sum(residual_diag)]
where the time goes in v1:
time: 41.2 us; the launch traced here: 40.9 us
  Pallas kernels  32 us (78%)
  local copies, waits for them, and re-layouts  8.24 us (20%)
  between operations  0.66 us (2%)
    pallas_call x1, Pallas kernels, body(): pl.pallas_call(functools.partial(body_kernel, n, blocks, chunk), name='wh...  32 us
    unnamed x7, local copies, waits for them, and re-layouts  4.24 us
    another operation x1, local copies, waits for them, and re-layouts, body(): flat.reshape(-1, 1)  1.4 us
    reshape x1, local copies, waits for them, and re-layouts, body(): scales.reshape(-1, 1)  1.32 us
    another operation x1, local copies, waits for them, and re-layouts, body(): flat.reshape(1, -1)  1.28 us

profile of v1, /device:TPU:0, one launch (start us, length us, event | category | flops | bytes accessed | tf_op | source)
XLA Modules:
  0.0 40.9 jit_solution(17521615105724355047)
XLA Ops:
  0.6 1.3 %reshape_reshape.6.pivot_row = s32[1,128]{1,0:T(1,128)} reshape(s32[8,16]{1,0:T(8,128)} %param.7) | data formatting | bytes 1024 | tf_op jit(solution)/shard_map/reshape;reshape | solution.py:245
  1.9 1.3 %copy.7.scales = f32[8,1]{1,0:T(8,128)} copy(f32[8,1]{0,1:T(1,128)} %bitcast.6) | data formatting | bytes 64 | tf_op jit(solution)/shard_map/reshape | solution.py:244
  3.2 1.4 %reshape_reshape.8.pivot_col = s32[128,1]{1,0:T(8,128)} reshape(s32[8,16]{1,0:T(8,128)} %param.7) | data formatting | bytes 1024 | tf_op jit(solution)/shard_map/reshape;reshape | solution.py:245
  4.6 32.0 %whole.1 = (f32[128,4096]{1,0:T(8,128)}, f32[1,4096]{1,0:T(1,128)}, f32[1,8]{1,0:T(1,128)}) custom-call(f32[8,4096]{1,0:T(8,128)} %points.1, f32[8,1]{1,0:T(8,128)} %copy.7.scales, f32[1,4096]{1,0:T(1,128)} %bitcast.5, s32[1,128]{1,0:T(1,128)} %reshape_reshape.6.pivot_row, s32[128,1]{1,0:T(8,128)} %reshape_reshape.8.pivot_col), custom_call_target="tpu_custom_call" | custom-call | tf_op jit(solution)/shard_map/whole/pallas_call | solution.py:219
  36.7 0.0 copy-start
  36.7 0.0 copy-start.1
  36.7 3.1 %copy.12 = f32[128,4096]{1,0:T(8,128)} copy(f32[128,4096]{1,0:T(8,128)} %get-tuple-element.12) | data formatting | bytes 4194304
  39.8 0.0 copy-done
  39.8 0.6 %copy.13 = f32[4096]{0:T(1024)} copy(f32[4096]{0:T(1024)S(1)} %bitcast.4) | data formatting | bytes 32768
  40.4 0.0 copy-done.1
  40.4 0.5 %copy.14 = f32[8]{0:T(128)} copy(f32[8]{0:T(128)S(1)} %bitcast.7) | data formatting | bytes 64
Async XLA Ops:
  36.7 3.1 %copy-start = (f32[1,4096]{1,0:T(1,128)S(1)}, f32[1,4096]{1,0:T(1,128)}, u32[]{:S(2)}) copy-start(f32[1,4096]{1,0:T(1,128)} %get-tuple-element.7) | copy-start | bytes 49156
  36.7 3.7 %copy-start.1 = (f32[1,8]{1,0:T(1,128)S(1)}, f32[1,8]{1,0:T(1,128)}, u32[]{:S(2)}) copy-start(f32[1,8]{1,0:T(1,128)} %get-tuple-element.8) | copy-start | bytes 100

commit v2 on v1

--- a/solution.py
+++ b/solution.py
@@ -22,13 +22,17 @@
 
 
 def load_points(dim, points, scales, noise, packed):
-    packed[0:dim, :] = points[...] / scales[...]
+    axis_pos = lax.broadcasted_iota(jnp.int32, (dim, 1), 0)
+    scale = jnp.ones((dim, 1), F32)
+    for d in range(dim):
+        scale = jnp.where(axis_pos == d, scales[d], scale)
+    packed[0:dim, :] = points[...] / scale
     packed[dim : 2 * dim, :] = jnp.broadcast_to(noise[...], (dim, noise.shape[1]))
 
 
 def gather_own(ranks, offset, chunk, pivot_row, packed):
     rows, width = packed.shape
-    wanted = pivot_row[...] - offset
+    wanted = pivot_row - offset
     acc = jnp.zeros((3 * rows, ranks), F32)
     for c in range(width // chunk):
         pieces = jnp.concatenate(split3(packed[:, c * chunk : (c + 1) * chunk]), axis=0)
@@ -134,7 +138,7 @@
 
 def body_kernel(
     n, blocks, chunk,
-    points, scales, noise, pivot_row, pivot_col,
+    points, scales, noise, pivots, unset_factor,
     factor, residual, averages,
     packed, slots, state, held, after, sum_slots,
     send_sem, recv_sem, sum_send_sem, sum_recv_sem, out_sem,
@@ -156,10 +160,14 @@
 
     lax.fori_loop(1, n, greet, 0)
     load_points(dim, points, scales, noise, packed)
-    slots[0] = gather_own(ranks, offset, chunk, pivot_row, packed)
+    pivot_row = jnp.concatenate([pivots[b : b + 1, :] for b in range(blocks)], axis=1)
+    own = gather_own(ranks, offset, chunk, pivot_row, packed)
+    for d in range(dim + 1):
+        slots[0, d] = own[d : d + 1]
     pl.semaphore_wait(barrier, n - 1)
     exchange_start(n, me, slots, send_sem, recv_sem)
     coords = exchange_finish(n, me, slots, send_sem, recv_sem)
+    coords = jnp.concatenate([coords[d] for d in range(dim + 1)], axis=0)
 
     cov, eye = pivot_covariance(dim, coords)
     state[:, 0:ranks] = cov
@@ -171,7 +179,8 @@
 
     centre = jnp.sum(coords[0:dim, :], axis=1, keepdims=True) / ranks
     side = pivot_side(dim, coords, centre)
-    local_col = pivot_col[...] - offset
+    local_row = (pivot_row - offset).astype(F32)
+    local_col = jnp.broadcast_to(local_row, (SUB, ranks)).T[:, 0:1].astype(jnp.int32)
     copies = []
     for c in range(width // chunk):
         at = slice(c * chunk, (c + 1) * chunk)
@@ -198,13 +207,13 @@
     total = jnp.zeros((blocks, LANES), F32)
     for c in range(width // LANES):
         total = total + after[:, c * LANES : (c + 1) * LANES]
-    sum_slots[0] = total
+    total = jnp.sum(total, axis=1, keepdims=True)
+    row = lax.broadcasted_iota(jnp.int32, (blocks, LANES), 0)
+    col = lax.broadcasted_iota(jnp.int32, (blocks, LANES), 1)
+    sum_slots[0] = jnp.sum(jnp.where(row == col, total, 0.0), axis=0, keepdims=True)
     exchange_start(n, me, sum_slots, sum_send_sem, sum_recv_sem)
     total = exchange_finish(n, me, sum_slots, sum_send_sem, sum_recv_sem)
-    total = jnp.sum(total, axis=1, keepdims=True) / (width * n)
-    row = lax.broadcasted_iota(jnp.int32, (blocks, LANES), 0)
-    col = lax.broadcasted_iota(jnp.int32, (blocks, LANES), 1)
-    averages[...] = jnp.sum(jnp.where(row == col, total, 0.0), axis=0, keepdims=True)[:, 0:blocks]
+    averages[...] = total[:, 0:blocks] / (width * n)
     for copy in copies:
         copy.wait()
 
@@ -215,7 +224,12 @@
     ranks = blocks * per_block
     chunk = 512
     vmem = pl.BlockSpec(memory_space=pltpu.VMEM)
-    flat = pivots.reshape(-1)
+    unset = pl.pallas_call(
+        lambda out: None,
+        name="unset",
+        out_shape=jax.ShapeDtypeStruct((ranks, width), F32),
+        out_specs=pl.BlockSpec(memory_space=pl.ANY),
+    )()
     factor, residual, averages = pl.pallas_call(
         functools.partial(body_kernel, n, blocks, chunk),
         name="whole",
@@ -224,15 +238,19 @@
             jax.ShapeDtypeStruct((1, width), F32),
             jax.ShapeDtypeStruct((1, blocks), F32),
         ),
-        in_specs=[vmem] * 5,
+        in_specs=[
+            vmem, pl.BlockSpec(memory_space=pltpu.SMEM), vmem, vmem,
+            pl.BlockSpec(memory_space=pl.ANY),
+        ],
+        input_output_aliases={4: 0},
         out_specs=(pl.BlockSpec(memory_space=pl.ANY), vmem, vmem),
         scratch_shapes=[
             pltpu.VMEM((2 * dim, width), F32),
-            pltpu.VMEM((n, 2 * dim, ranks), F32),
+            pltpu.VMEM((n, dim + 1, 1, ranks), F32),
             pltpu.VMEM((ranks, 2 * ranks), F32),
             pltpu.VMEM((ranks, width), F32),
             pltpu.VMEM((blocks, width), F32),
-            pltpu.VMEM((n, blocks, LANES), F32),
+            pltpu.VMEM((n, 1, LANES), F32),
             pltpu.SemaphoreType.DMA((n,)),
             pltpu.SemaphoreType.DMA((n,)),
             pltpu.SemaphoreType.DMA((n,)),
@@ -240,10 +258,7 @@
             pltpu.SemaphoreType.DMA((width // chunk,)),
         ],
         compiler_params=pltpu.CompilerParams(collective_id=0, has_side_effects=True),
-    )(
-        points, scales.reshape(-1, 1), noise_var.reshape(1, -1),
-        flat.reshape(1, -1), flat.reshape(-1, 1),
-    )
+    )(points, scales, noise_var.reshape(1, -1), pivots, unset)
     return factor, residual.reshape(-1), averages.reshape(-1)
 
 

time: 41.2 us -> 34.7 us (0.84)
  local copies, waits for them, and re-layouts: 8.24 us -> 4.24 us
  Pallas kernels: 32 us -> 29.6 us
    another operation x2 -> x0, local copies, waits for them, and re-layouts: 2.68 us -> none  [the longest x1 1.4 us: body(): flat.reshape(-1, 1)]
    pallas_call x1, Pallas kernels: 32 us -> 29.6 us  [body(): pl.pallas_call(functools.partial(body_kernel, n, blocks, chunk), name='wh...]
    reshape x1 -> x0, local copies, waits for them, and re-layouts: 1.32 us -> none  [body(): scales.reshape(-1, 1)]
where the time goes in v2:
time: 34.7 us; the launch traced here: 34.5 us
  Pallas kernels  29.6 us (85%)
  local copies, waits for them, and re-layouts  4.24 us (12%)
  between operations  0.66 us (2%)
    pallas_call x1, Pallas kernels, body(): pl.pallas_call(functools.partial(body_kernel, n, blocks, chunk), name='wh...  29.6 us
    unnamed x7, local copies, waits for them, and re-layouts  4.24 us

profile of v2, /device:TPU:0, one launch (start us, length us, event | category | flops | bytes accessed | tf_op | source)
XLA Modules:
  0.0 34.5 jit_solution(8406201685613649031)
XLA Ops:
  0.6 29.6 %whole.1 = (f32[128,4096]{1,0:T(8,128)}, f32[1,4096]{1,0:T(1,128)}, f32[1,8]{1,0:T(1,128)}) custom-call(f32[8,4096]{1,0:T(8,128)} %points.1, f32[8]{0:T(128)} %scales.1, f32[1,4096]{1,0:T(1,128)} %bitcast.3, s32[8,16]{1,0:T(8,128)} %pivots.1, f32[128,4096]{1,0:T(8,128)} %unset.1.unset_factor), custom_call_target="tpu_custom_call", output_to_operand_aliasing={{0}: (4, {})} | custom-call | tf_op jit(solution)/shard_map/whole/pallas_call | solution.py:233
  30.3 0.0 copy-start
  30.3 0.0 copy-start.1
  30.3 3.1 %copy.12 = f32[128,4096]{1,0:T(8,128)} copy(f32[128,4096]{1,0:T(8,128)} %get-tuple-element.12) | data formatting | bytes 4194304
  33.4 0.0 copy-done
  33.4 0.6 %copy.13 = f32[4096]{0:T(1024)} copy(f32[4096]{0:T(1024)S(1)} %bitcast.4) | data formatting | bytes 32768
  34.0 0.0 copy-done.1
  34.0 0.5 %copy.14 = f32[8]{0:T(128)} copy(f32[8]{0:T(128)S(1)} %bitcast.5) | data formatting | bytes 64
  (1 shorter events, 0.0 us)
Async XLA Ops:
  30.3 3.1 %copy-start = (f32[1,4096]{1,0:T(1,128)S(1)}, f32[1,4096]{1,0:T(1,128)}, u32[]{:S(2)}) copy-start(f32[1,4096]{1,0:T(1,128)} %get-tuple-element.7) | copy-start | bytes 49156
  30.3 3.7 %copy-start.1 = (f32[1,8]{1,0:T(1,128)S(1)}, f32[1,8]{1,0:T(1,128)}, u32[]{:S(2)}) copy-start(f32[1,8]{1,0:T(1,128)} %get-tuple-element.8) | copy-start | bytes 100

commit v3 on v2

--- a/solution.py
+++ b/solution.py
@@ -85,28 +85,65 @@
     return cov, (row == col).astype(F32)
 
 
+def eliminate(left, right, first_lane):
+    shape = left[0].shape
+    a = [
+        [
+            jnp.broadcast_to(left[i][:, first_lane + j : first_lane + j + 1], shape)
+            for j in range(i + 1)
+        ]
+        for i in range(SUB)
+    ]
+    inverse = []
+    for k in range(SUB):
+        r = lax.rsqrt(a[k][k])
+        inverse.append(r)
+        left[k] = left[k] * r
+        right[k] = right[k] * r
+        for i in range(k + 1, SUB):
+            a[i][k] = a[i][k] * r
+        for i in range(k + 1, SUB):
+            for j in range(k + 1, i + 1):
+                a[i][j] = a[i][j] - a[i][k] * a[j][k]
+            left[i] = left[i] - a[i][k] * left[k]
+            right[i] = right[i] - a[i][k] * right[k]
+    return a, inverse
+
+
+def spread(rows):
+    return [jnp.broadcast_to(rows[i : i + 1], rows.shape) for i in range(SUB)]
+
+
+def gathered(rows):
+    return jnp.concatenate([rows[i][i : i + 1] for i in range(SUB)], axis=0)
+
+
 def factor_rows(ranks, state):
-    for b in range(ranks // SUB):
-        lo, hi = b * SUB, (b + 1) * SUB
-        left = [state[lo + i : lo + i + 1, 0:ranks] for i in range(SUB)]
-        right = [state[lo + i : lo + i + 1, ranks : 2 * ranks] for i in range(SUB)]
-        a = [
-            [jnp.broadcast_to(left[i][:, lo + j : lo + j + 1], (1, ranks)) for j in range(i + 1)]
-            for i in range(SUB)
+    step = 2 * SUB
+    for lo in range(0, ranks, step):
+        mid, hi = lo + SUB, lo + step
+        left = spread(state[lo:mid, 0:ranks])
+        right = spread(state[lo:mid, ranks : 2 * ranks])
+        low_left = state[mid:hi, 0:ranks]
+        low_right = state[mid:hi, ranks : 2 * ranks]
+        start = [
+            jnp.broadcast_to(low_left[:, lo + k : lo + k + 1], (SUB, ranks))
+            for k in range(SUB)
         ]
+        mult, inverse = eliminate(left, right, lo)
+        cols = []
         for k in range(SUB):
-            r = lax.rsqrt(a[k][k])
-            left[k] = left[k] * r
-            right[k] = right[k] * r
-            mult = {i: a[i][k] * r for i in range(k + 1, SUB)}
-            for i in range(k + 1, SUB):
-                for j in range(k + 1, i + 1):
-                    a[i][j] = a[i][j] - mult[i] * mult[j]
-                left[i] = left[i] - mult[i] * left[k]
-                right[i] = right[i] - mult[i] * right[k]
-        new_left = jnp.concatenate(left, axis=0)
-        new_right = jnp.concatenate(right, axis=0)
-        state[lo:hi, 0:ranks] = new_left
+            col = start[k]
+            for j in range(k):
+                col = col - cols[j] * mult[k][j]
+            cols.append(col * inverse[k])
+        for k in range(SUB):
+            low_left = low_left - cols[k] * left[k]
+            low_right = low_right - cols[k] * right[k]
+        next_left, next_right = spread(low_left), spread(low_right)
+        eliminate(next_left, next_right, mid)
+        new_left = jnp.concatenate([gathered(left), gathered(next_left)], axis=0)
+        new_right = jnp.concatenate([gathered(right), gathered(next_right)], axis=0)
         state[lo:hi, ranks : 2 * ranks] = new_right
         if hi < ranks:
             new = jnp.concatenate([new_left, new_right], axis=1)
@@ -138,13 +175,13 @@
 
 def body_kernel(
     n, blocks, chunk,
-    points, scales, noise, pivots, unset_factor,
+    points, scales, noise, pivots,
     factor, residual, averages,
-    packed, slots, state, held, after, sum_slots,
-    send_sem, recv_sem, sum_send_sem, sum_recv_sem, out_sem,
+    packed, slots, state, after, sum_slots,
+    send_sem, recv_sem, sum_send_sem, sum_recv_sem,
 ):
     dim, width = points.shape
-    ranks = held.shape[0]
+    ranks = factor.shape[0]
     per_block = ranks // blocks
     me = lax.axis_index("rows")
     offset = me * width
@@ -181,7 +218,6 @@
     side = pivot_side(dim, coords, centre)
     local_row = (pivot_row - offset).astype(F32)
     local_col = jnp.broadcast_to(local_row, (SUB, ranks)).T[:, 0:1].astype(jnp.int32)
-    copies = []
     for c in range(width // chunk):
         at = slice(c * chunk, (c + 1) * chunk)
         x = packed[0:dim, at] - centre
@@ -192,17 +228,13 @@
         rows = jnp.dot(
             solve, cross, precision=lax.Precision.HIGHEST, preferred_element_type=F32
         )
-        held[:, at] = rows
-        copies.append(
-            pltpu.make_async_copy(held.at[:, at], factor.at[:, at], out_sem.at[c])
-        )
-        copies[-1].start()
+        factor[:, at] = rows
         left = 1.0 + noise_row
         for b in range(blocks):
             part = rows[b * per_block : (b + 1) * per_block]
             left = left - jnp.sum(part * part, axis=0, keepdims=True)
             after[b : b + 1, at] = left
-        residual[:, at] = left
+        residual[at] = left[0]
 
     total = jnp.zeros((blocks, LANES), F32)
     for c in range(width // LANES):
@@ -213,7 +245,18 @@
     sum_slots[0] = jnp.sum(jnp.where(row == col, total, 0.0), axis=0, keepdims=True)
     exchange_start(n, me, sum_slots, sum_send_sem, sum_recv_sem)
     total = exchange_finish(n, me, sum_slots, sum_send_sem, sum_recv_sem)
-    averages[...] = total[:, 0:blocks] / (width * n)
+    averages[...] = total[0, 0:blocks] / (width * n)
+
+
+def store_kernel(factor, residual, averages, to_factor, to_residual, to_averages, sem):
+    copies = [
+        pltpu.make_async_copy(source, target, sem.at[i])
+        for i, (source, target) in enumerate(
+            [(factor, to_factor), (residual, to_residual), (averages, to_averages)]
+        )
+    ]
+    for copy in copies:
+        copy.start()
     for copy in copies:
         copy.wait()
 
@@ -224,42 +267,44 @@
     ranks = blocks * per_block
     chunk = 512
     vmem = pl.BlockSpec(memory_space=pltpu.VMEM)
-    unset = pl.pallas_call(
-        lambda out: None,
-        name="unset",
-        out_shape=jax.ShapeDtypeStruct((ranks, width), F32),
-        out_specs=pl.BlockSpec(memory_space=pl.ANY),
-    )()
     factor, residual, averages = pl.pallas_call(
         functools.partial(body_kernel, n, blocks, chunk),
         name="whole",
         out_shape=(
-            jax.ShapeDtypeStruct((ranks, width), F32),
-            jax.ShapeDtypeStruct((1, width), F32),
-            jax.ShapeDtypeStruct((1, blocks), F32),
+            pltpu.VMEM((ranks, width), F32),
+            pltpu.VMEM((width,), F32),
+            pltpu.VMEM((blocks,), F32),
         ),
         in_specs=[
             vmem, pl.BlockSpec(memory_space=pltpu.SMEM), vmem, vmem,
-            pl.BlockSpec(memory_space=pl.ANY),
         ],
-        input_output_aliases={4: 0},
-        out_specs=(pl.BlockSpec(memory_space=pl.ANY), vmem, vmem),
+        out_specs=(vmem, vmem, vmem),
         scratch_shapes=[
             pltpu.VMEM((2 * dim, width), F32),
             pltpu.VMEM((n, dim + 1, 1, ranks), F32),
             pltpu.VMEM((ranks, 2 * ranks), F32),
-            pltpu.VMEM((ranks, width), F32),
             pltpu.VMEM((blocks, width), F32),
             pltpu.VMEM((n, 1, LANES), F32),
             pltpu.SemaphoreType.DMA((n,)),
             pltpu.SemaphoreType.DMA((n,)),
             pltpu.SemaphoreType.DMA((n,)),
             pltpu.SemaphoreType.DMA((n,)),
-            pltpu.SemaphoreType.DMA((width // chunk,)),
         ],
         compiler_params=pltpu.CompilerParams(collective_id=0, has_side_effects=True),
-    )(points, scales, noise_var.reshape(1, -1), pivots, unset)
-    return factor, residual.reshape(-1), averages.reshape(-1)
+    )(points, scales, noise_var.reshape(1, -1), pivots)
+    anywhere = pl.BlockSpec(memory_space=pl.ANY)
+    return pl.pallas_call(
+        store_kernel,
+        name="store",
+        out_shape=(
+            jax.ShapeDtypeStruct((ranks, width), F32),
+            jax.ShapeDtypeStruct((width,), F32),
+            jax.ShapeDtypeStruct((blocks,), F32),
+        ),
+        in_specs=[vmem] * 3,
+        out_specs=(anywhere,) * 3,
+        scratch_shapes=[pltpu.SemaphoreType.DMA((3,))],
+    )(*(pltpu.with_memory_space_constraint(x, pltpu.VMEM) for x in (factor, residual, averages)))
 
 
 def solution(mesh):

time: 34.7 us -> 30.1 us (0.87)
  local copies, waits for them, and re-layouts: 4.24 us -> 0 us
    unnamed x7 -> x0, local copies, waits for them, and re-layouts: 4.24 us -> none
    pallas_call x1, Pallas kernels: 29.6 us -> 28 us  [body(): pl.pallas_call(functools.partial(body_kernel, n, blocks, chunk), name='wh...]
    pallas_call x1, Pallas kernels: 0.01 us -> 1.35 us  [body(): pl.pallas_call(store_kernel, name='store', out_shape=(jax.ShapeDtypeStruc...]
where the time goes in v3:
time: 30.1 us; the launch traced here: 29.9 us
  Pallas kernels  29.3 us (97%)
  between operations  0.64 us (2%)
    pallas_call x1, Pallas kernels, body(): pl.pallas_call(functools.partial(body_kernel, n, blocks, chunk), name='wh...  28 us
    pallas_call x1, Pallas kernels, body(): pl.pallas_call(store_kernel, name='store', out_shape=(jax.ShapeDtypeStruc...  1.35 us

profile of v3, /device:TPU:0, one launch (start us, length us, event | category | flops | bytes accessed | tf_op | source)
XLA Modules:
  0.0 29.9 jit_solution(16096990109169777456)
XLA Ops:
  0.6 28.0 %whole.1 = (f32[128,4096]{1,0:T(8,128)S(1)}, f32[4096]{0:T(1024)S(1)}, f32[8]{0:T(128)S(1)}) custom-call(f32[8,4096]{1,0:T(8,128)} %points.1, f32[8]{0:T(128)} %scales.1, f32[1,4096]{1,0:T(1,128)} %bitcast.1, s32[8,16]{1,0:T(8,128)} %pivots.1), custom_call_target="tpu_custom_call" | custom-call | tf_op jit(solution)/shard_map/whole/pallas_call | solution.py:270
  28.6 1.4 %store.1 = (f32[128,4096]{1,0:T(8,128)}, f32[4096]{0:T(1024)}, f32[8]{0:T(128)}) custom-call(f32[128,4096]{1,0:T(8,128)S(1)} %get-tuple-element.6.factor, f32[4096]{0:T(1024)S(1)} %get-tuple-element.7.residual, f32[8]{0:T(128)S(1)} %get-tuple-element.8.averages), custom_call_target="tpu_custom_call" | custom-call | tf_op jit(solution)/shard_map/store/pallas_call | solution.py:296
